TPU v7x, 256 devices: a whole 4x4x8 slice. The times are simulated.
256 devices in a mesh: rows: 4 (over x), grid: 64 (over z, y, core).
Axes of the slice: x: 4, y: 4, z: 8, core: 2. Of those that a mesh axis runs over, the one named last changes fastest.
Arguments:
- positions: int32 [2, 2048], P(None, 'rows'), may hold values from 0 to 63, as said below
- angles: int32 [2, 32768], P(None, 'grid'), may hold values from 0 to 4095
- subspace: bfloat16 [2, 2048, 1920], P(None, 'rows', 'grid')
Outputs:
- spectrum: float32 [32768], P('grid')
Inputs may be any that keep to these rules, and one draw needn't show every extreme that they name: `positions`: each column names a distinct lattice point; both coordinates lie in 0 to 63.
All inputs are finite; a program needn't handle non-finite values.
Results may differ from a plain program's by a relative error of at most 0.0012.
Values may be sent and summed in bfloat16 or wider, within the bound.
No kernel may reach another device: no remote copies, remote signals or barrier semaphores. Data moves between devices by JAX's collectives and lax.ppermute only.
A program may use at most 64 MiB of HBM per device.

v0:
```python
import jax
import jax.numpy as jnp
import numpy as np
from jax import lax
from jax.experimental import pallas as pl
from jax.experimental.pallas import tpu as pltpu
from jax.sharding import Mesh
from jax.sharding import PartitionSpec as P

NOISE = 1920
PHASES = 4096
LATTICE = 64
LANES = 128
BATCH = 32
PITCH = BATCH + 4
ROWS, FAR, NEAR, SIDE, CORE = "rows", "far", "near", "side", "core"
GRID = (FAR, NEAR, SIDE, CORE)


def sine_coefficients():
    nodes = 0.03125 * (1.0 - np.cos((np.arange(64) + 0.5) * np.pi / 64))
    root = np.sqrt(nodes)
    value = np.sin(2.0 * np.pi * root) / root
    return tuple(float(c) for c in np.polynomial.polynomial.polyfit(nodes, value, 5))


SINE = sine_coefficients()


def sine_of(u):
    square = u * u
    total = jnp.full_like(u, SINE[-1])
    for c in SINE[-2::-1]:
        total = total * square + c
    return total * u


def cos_sin_of(turns):
    rest = turns - jnp.round(turns)
    cos = sine_of(0.25 - jnp.abs(rest))
    sin = sine_of(jnp.maximum(jnp.minimum(rest, 0.5 - rest), -0.5 - rest))
    return cos, sin


def pack_kernel(positions_hbm, angles_hbm, columns_hbm, out_ref, turns_ref, positions, angles, columns, sems):
    pairs = ((positions_hbm, positions), (angles_hbm, angles), (columns_hbm, columns))
    copies = [pltpu.make_async_copy(*pair, sems.at[k]) for k, pair in enumerate(pairs)]
    for copy in copies:
        copy.start()
    for copy in copies:
        copy.wait()
    row_groups, far, tiles = out_ref.shape[0], out_ref.shape[1], positions.shape[0]
    quarter, width = (out_ref.shape[2] - 1) // tiles, columns.shape[0]
    turns_ref[...] = angles[...].astype(jnp.float32) * (1.0 / PHASES)
    mine = positions[lax.axis_index(FAR)].astype(jnp.float32).astype(out_ref.dtype)
    nothing = jnp.zeros((2, LANES), out_ref.dtype)
    for r in range(row_groups):
        for c in range(quarter):
            column = r * quarter + c
            for t in range(tiles):
                part = columns[column, :, t * LANES : (t + 1) * LANES] if column < width else nothing
                for d in range(far):
                    out_ref[r, d, t * quarter + c] = part
        for d in range(far):
            out_ref[r, d, tiles * quarter] = mine


def packed(positions, angles, columns, row_groups, far):
    width, tiles = columns.shape[0], positions.shape[0]
    assert tiles == far
    pairs = tiles * -(-width // row_groups) + 1
    return pl.pallas_call(
        pack_kernel,
        out_shape=(
            jax.ShapeDtypeStruct((row_groups, far, pairs, 2, LANES), columns.dtype),
            jax.ShapeDtypeStruct(angles.shape, jnp.float32),
        ),
        in_specs=[pl.BlockSpec(memory_space=pltpu.HBM)] * 3,
        out_specs=[pl.BlockSpec(memory_space=pltpu.VMEM)] * 2,
        scratch_shapes=[
            pltpu.VMEM(positions.shape, positions.dtype),
            pltpu.VMEM(angles.shape, angles.dtype),
            pltpu.VMEM(columns.shape, columns.dtype),
            pltpu.SemaphoreType.DMA((3,)),
        ],
        cost_estimate=pl.CostEstimate(flops=2**16, bytes_accessed=0, transcendentals=0),
        compiler_params=pltpu.CompilerParams(vmem_limit_bytes=2 * 2**20),
        name="pack",
    )(*(pltpu.with_memory_space_constraint(part, pltpu.HBM) for part in (positions, angles, columns)))


def tables_kernel(*refs):
    *parts, table_ref, turns = refs
    side, share = len(parts), parts[0].shape[1]
    blocks = turns.shape[1]
    each = share // LANES
    for s, ref in enumerate(parts):
        first = lax.rem(lax.axis_index(SIDE) + side - s, side) * each
        part = ref[...]
        for j in range(each):
            for k in range(2):
                turns[k, pl.ds(first + j, 1), :] = part[k : k + 1, j * LANES : (j + 1) * LANES]

    def fill(step, carry):
        for k in range(2):
            cos, sin = cos_sin_of(turns[k] * step.astype(jnp.float32))
            first = pl.multiple_of(2 * step * blocks, 2 * blocks)
            table_ref[k, pl.ds(first, blocks), :] = cos
            table_ref[k, pl.ds(first + blocks, blocks), :] = sin
        return carry

    lax.fori_loop(0, LATTICE, fill, 0, unroll=4)


def tables_of(parts):
    blocks = len(parts) * parts[0].shape[1] // LANES
    return pl.pallas_call(
        tables_kernel,
        out_shape=jax.ShapeDtypeStruct((2, LATTICE * 2 * blocks, LANES), jnp.float32),
        in_specs=[pl.BlockSpec(memory_space=pltpu.VMEM)] * len(parts),
        out_specs=pl.BlockSpec(memory_space=pltpu.VMEM),
        scratch_shapes=[pltpu.VMEM((2, blocks, LANES), jnp.float32)],
        cost_estimate=pl.CostEstimate(flops=2**22, bytes_accessed=0, transcendentals=0),
        compiler_params=pltpu.CompilerParams(vmem_limit_bytes=4 * 2**20),
        name="tables",
    )(*parts)


def steering_kernel(own_ref, table_ref, out_ref, stage, listed, rows, arrived):
    row_groups, tiles, pairs, _, _ = own_ref.shape
    blocks, elements = out_ref.shape[1:3]
    for r in range(row_groups):
        for t in range(tiles):
            part = (own_ref[r, t, pairs - 1].astype(jnp.float32) * (2 * blocks)).astype(jnp.int32)
            for k in range(2):
                here = k * elements + (r * tiles + t) * LANES
                listed[here : here + LANES] = part[k]
    copy = pltpu.make_async_copy(listed, rows, arrived)
    copy.start()
    copy.wait()

    def batch(step, carry):
        first = pl.multiple_of(step * BATCH, BATCH)
        for e in range(BATCH):
            one = pl.multiple_of(rows[first + e], 2 * blocks)
            two = pl.multiple_of(rows[elements + first + e], 2 * blocks)
            cos_one, sin_one = jnp.split(table_ref[0, pl.ds(one, 2 * blocks), :], 2)
            cos_two, sin_two = jnp.split(table_ref[1, pl.ds(two, 2 * blocks), :], 2)
            here = pl.ds(e, blocks, stride=PITCH)
            stage[0, here, :] = cos_one * cos_two - sin_one * sin_two
            stage[1, here, :] = sin_one * cos_two + cos_one * sin_two
        for k in range(2):
            for b in range(blocks):
                part = stage[k, b * PITCH : b * PITCH + BATCH, :]
                out_ref[k, b, pl.ds(first, BATCH), :] = part.astype(out_ref.dtype)
        return carry

    lax.fori_loop(0, elements // BATCH, batch, 0)


def steering_of(own, table):
    blocks = table.shape[1] // (2 * LATTICE)
    elements = own.shape[0] * own.shape[1] * LANES
    return pl.pallas_call(
        steering_kernel,
        out_shape=pltpu.VMEM((2, blocks, elements, LANES), own.dtype),
        in_specs=[pl.BlockSpec(memory_space=pltpu.VMEM)] * 2,
        out_specs=pl.BlockSpec(memory_space=pltpu.VMEM),
        scratch_shapes=[
            pltpu.VMEM((2, blocks * PITCH, LANES), jnp.float32),
            pltpu.VMEM((2 * elements,), jnp.int32),
            pltpu.SMEM((2 * elements,), jnp.int32),
            pltpu.SemaphoreType.DMA,
        ],
        cost_estimate=pl.CostEstimate(
            flops=64 * blocks * elements * LANES, bytes_accessed=0, transcendentals=0
        ),
        compiler_params=pltpu.CompilerParams(vmem_limit_bytes=6 * 2**20),
        name="steering",
    )(own, table)


def sums_kernel(*refs):
    *pieces, steering_ref, out_ref = refs
    row_groups, far, pairs, _, _ = pieces[0].shape
    tiles = steering_ref.shape[2] // (row_groups * LANES)
    quarter = (pairs - 1) // tiles
    weights = [
        [
            ref[r, d, t * quarter : (t + 1) * quarter].reshape(2 * quarter, LANES)
            for r in range(row_groups)
            for t in range(tiles)
        ]
        for ref in pieces
        for d in range(far)
    ]
    weights = jnp.concatenate([jnp.concatenate(part, 1) for part in weights], 0)
    is_real = lax.broadcasted_iota(jnp.int32, (8, LANES), 0) % 2 == 0
    for b in range(out_ref.shape[0]):
        both = jnp.concatenate([steering_ref[0, b], steering_ref[1, b]], 1)
        product = jnp.dot(weights, both, preferred_element_type=jnp.float32)
        total = jnp.zeros((8, LANES), jnp.float32)
        for g in range(0, product.shape[0], 8):
            cos, sin = product[g : g + 8, :LANES], product[g : g + 8, LANES:]
            real = cos + pltpu.roll(sin, 7, 0)
            imag = sin - pltpu.roll(cos, 7, 0)
            total = total + (real * real + imag * imag)
        out_ref[b : b + 1, :] = jnp.sum(jnp.where(is_real, total, 0.0), 0, keepdims=True)


def sums_of(pieces, steering):
    blocks = steering.shape[1]
    return pl.pallas_call(
        sums_kernel,
        out_shape=jax.ShapeDtypeStruct((blocks, LANES), jnp.float32),
        in_specs=[pl.BlockSpec(memory_space=pltpu.VMEM)] * (len(pieces) + 1),
        out_specs=pl.BlockSpec(memory_space=pltpu.VMEM),
        cost_estimate=pl.CostEstimate(
            flops=8 * len(pieces) * pieces[0].size * blocks * LANES,
            bytes_accessed=0,
            transcendentals=0,
        ),
        compiler_params=pltpu.CompilerParams(vmem_limit_bytes=6 * 2**20),
        name="sums",
    )(*pieces, steering)


def spectrum_of(positions, angles, subspace):
    rows, side, far = lax.axis_size(ROWS), lax.axis_size(SIDE), lax.axis_size(FAR)
    tiles = positions.shape[1] // LANES
    coordinates = positions.reshape(2, tiles, LANES).transpose(1, 0, 2)
    pieces, turns = packed(coordinates, angles, subspace.transpose(2, 0, 1), rows, far)
    own = lax.all_to_all(
        pieces.reshape(rows * far, *pieces.shape[2:]), (ROWS, FAR), 0, 0, tiled=True
    )
    turned = [turns]
    for step in range(1, side):
        moves = [(s, (s + step) % side) for s in range(side)]
        turned.append(lax.ppermute(turns, SIDE, moves))
    cores = [(0, 1), (1, 0)]
    along = lax.ppermute(own, NEAR, [(0, 1), (1, 0)])
    across = lax.ppermute(own, CORE, cores)
    both = lax.ppermute(along, CORE, cores)
    own, *shared = (part.reshape(pieces.shape) for part in (own, along, across, both))

    steering = steering_of(own, tables_of(turned))
    sums = sums_of((own, *shared), steering).reshape(1, side, -1)
    sums = jnp.broadcast_to(sums, (rows, *sums.shape[1:]))
    parts = lax.all_to_all(sums.reshape(rows * side, -1), (ROWS, SIDE), 0, 0, tiled=True)
    return 1.0 / (jnp.sum(parts, 0) / NOISE + 1e-06)


def solution(mesh):
    split = Mesh(mesh.devices.reshape(mesh.shape["rows"], 4, 2, 4, 2), (ROWS, *GRID))
    in_specs = (P(None, ROWS), P(None, GRID), P(None, ROWS, GRID))
    return jax.shard_map(spectrum_of, mesh=split, in_specs=in_specs, out_specs=P(GRID), check_vma=False)
```

profile of v0, /device:TPU:8, one launch (start us, length us, event | category | flops | bytes accessed | tf_op | source)
XLA Modules:
  0.0 64.5 jit_solution(10702708166566886544)
XLA Ops:
  0.0 1.0 %pack.1 = (bf16[4,4,33,2,128]{4,3,2,1,0:T(2,128)(2,1)S(1)}, f32[2,512]{1,0:T(2,128)S(1)}) custom-call(s32[4,2,128]{2,1,0:T(2,128)} %bitcast.16, s32[2,512]{1,0:T(2,128)} %angles_hbm.1, bf16[30,2,512]{2,1,0:T(2,128)(2,1)} %bitcast.15), custom_call_target="tpu_custom_call" | custom-call | flops 65536 | tf_op jit(solution)/shard_map/pack/pallas_call | solution.py:72
  1.0 24.3 %all_to_all.14 = bf16[16,33,2,128]{3,2,1,0:T(2,128)(2,1)S(1)} all-to-all(bf16[16,33,2,128]{3,2,1,0:T(2,128)(2,1)S(1)} %bitcast.11), channel_id=1, replica_groups=mesh['rows'=4,'far'=4,'near'=2,'side'=4,'core'=2] {'rows','far'}, dimensions={0} | all-to-all | bytes 540672 | tf_op jit(solution)/shard_map/all_to_all | solution.py:233
  25.3 1.1 %collective-permute-start = (bf16[16,33,2,128]{3,2,1,0:T(2,128)(2,1)S(1)}, bf16[16,33,2,128]{3,2,1,0:T(2,128)(2,1)S(1)}, u32[]{:S(2)}, u32[]{:S(2)}) collective-permute-start(bf16[16,33,2,128]{3,2,1,0:T(2,128)(2,1)S(1)} %all_to_all.14), channel_id=1, source_target_pairs={{0,8},{8,0},{1,9},{9,1},{2,10},{10,2},{3,11},{11,3},{4,12},{12,4},... | collective-permute-start | bytes 811016 | tf_op jit(solution)/shard_map/ppermute | solution.py:241
  26.4 0.0 collective-permute-start.1
  26.4 6.0 %collective-permute-done = bf16[16,33,2,128]{3,2,1,0:T(2,128)(2,1)S(1)} collective-permute-done((bf16[16,33,2,128]{3,2,1,0:T(2,128)(2,1)S(1)}, bf16[16,33,2,128]{3,2,1,0:T(2,128)(2,1)S(1)}, u32[]{:S(2)}, u32[]{:S(2)}) %collective-permute-start) | collective-permute-done | bytes 270368 | tf_op jit(solution)/shard_map/ppermute | solution.py:241
  32.4 0.0 collective-permute-start.2
  32.4 1.6 %collective-permute-start.3 = (f32[2,512]{1,0:T(2,128)S(1)}, f32[2,512]{1,0:T(2,128)S(1)}, u32[]{:S(2)}, u32[]{:S(2)}) collective-permute-start(f32[2,512]{1,0:T(2,128)S(1)} %get-tuple-element.8.refs_0_), channel_id=1, source_target_pairs={{0,2},{2,4},{4,6},{6,0},{1,3},{3,5},{5,7},{7,1},{8,10},{10,12},{12... | collective-permute-start | bytes 12296 | tf_op jit(solution)/shard_map/ppermute | solution.py:239
  34.0 0.9 %collective-permute-start.4 = (f32[2,512]{1,0:T(2,128)S(1)}, f32[2,512]{1,0:T(2,128)S(1)}, u32[]{:S(2)}, u32[]{:S(2)}) collective-permute-start(f32[2,512]{1,0:T(2,128)S(1)} %get-tuple-element.8.refs_0_), channel_id=1, source_target_pairs={{0,4},{2,6},{4,0},{6,2},{1,5},{3,7},{5,1},{7,3},{8,12},{10,14},{12... | collective-permute-start | bytes 12296 | tf_op jit(solution)/shard_map/ppermute | solution.py:239
  34.9 2.4 %collective-permute-start.5 = (f32[2,512]{1,0:T(2,128)S(1)}, f32[2,512]{1,0:T(2,128)S(1)}, u32[]{:S(2)}, u32[]{:S(2)}) collective-permute-start(f32[2,512]{1,0:T(2,128)S(1)} %get-tuple-element.8.refs_0_), channel_id=1, source_target_pairs={{0,6},{2,0},{4,2},{6,4},{1,7},{3,1},{5,3},{7,5},{8,14},{10,8},{12,... | collective-permute-start | bytes 12296 | tf_op jit(solution)/shard_map/ppermute | solution.py:239
  37.3 0.0 collective-permute-done.3.refs_1_
  37.3 1.8 %collective-permute-done.4.refs_2_ = f32[2,512]{1,0:T(2,128)S(1)} collective-permute-done((f32[2,512]{1,0:T(2,128)S(1)}, f32[2,512]{1,0:T(2,128)S(1)}, u32[]{:S(2)}, u32[]{:S(2)}) %collective-permute-start.4) | collective-permute-done | bytes 4128 | tf_op jit(solution)/shard_map/ppermute | solution.py:239
  39.1 0.0 collective-permute-done.5.refs_3_
  39.1 1.3 %tables.1.table_ref = f32[2,2048,128]{2,1,0:T(8,128)S(1)} custom-call(f32[2,512]{1,0:T(2,128)S(1)} %get-tuple-element.8.refs_0_, f32[2,512]{1,0:T(2,128)S(1)} %collective-permute-done.3.refs_1_, f32[2,512]{1,0:T(2,128)S(1)} %collective-permute-done.4.refs_2_, f32[2,512]{1,0:T(2,128)S(1)} %collective-permute-done.5.refs_3_), custom_call_target="tpu_custom_call" | custom-call | flops 4194304 | tf_op jit(solution)/shard_map/tables/pallas_call | solution.py:117
  40.4 6.7 %steering.1.refs_4_ = bf16[2,16,2048,128]{3,2,1,0:T(8,128)(2,1)S(1)} custom-call(bf16[4,4,33,2,128]{4,3,2,1,0:T(2,128)(2,1)S(1)} %bitcast.9, f32[2,2048,128]{2,1,0:T(8,128)S(1)} %tables.1.table_ref), custom_call_target="tpu_custom_call" | custom-call | flops 268435456 | tf_op jit(solution)/shard_map/steering/pallas_call | solution.py:164
  47.1 0.0 collective-permute-done.1
  47.1 0.0 collective-permute-done.2
  47.1 4.7 %sums.1 = f32[16,128]{1,0:T(8,128)S(1)} custom-call(bf16[4,4,33,2,128]{4,3,2,1,0:T(2,128)(2,1)S(1)} %bitcast.10, bf16[4,4,33,2,128]{4,3,2,1,0:T(2,128)(2,1)S(1)} %bitcast.12, bf16[4,4,33,2,128]{4,3,2,1,0:T(2,128)(2,1)S(1)} %bitcast.13, bf16[4,4,33,2,128]{4,3,2,1,0:T(2,128)(2,1)S(1)} %bitcast.14, bf16[2,16,2048,128]{3,2,1,0:T(8,128)(2,1)S(1)} %steering.1.refs_4_), custom_call_target="tpu_custom_call" | custom-call | flops 8858370048 | tf_op jit(solution)/shard_map/sums/pallas_call | solution.py:213
  51.8 0.1 all_to_all.10
  51.8 12.0 %all_to_all.15 = f32[16,1,512]{2,1,0:T(1,128)S(1)} all-to-all(f32[16,1,512]{2,1,0:T(1,128)S(1)} %all_to_all.10), channel_id=1, replica_groups=mesh['rows'=4,'far'=4,'near'=2,'side'=4,'core'=2] {'rows','side'}, dimensions={0} | all-to-all | bytes 65536 | tf_op jit(solution)/shard_map/all_to_all | solution.py:249
  63.9 0.6 add_divide_fusion
  (3 shorter events, 0.1 us)
Async XLA Ops:
  25.3 7.1 %collective-permute-start = (bf16[16,33,2,128]{3,2,1,0:T(2,128)(2,1)S(1)}, bf16[16,33,2,128]{3,2,1,0:T(2,128)(2,1)S(1)}, u32[]{:S(2)}, u32[]{:S(2)}) collective-permute-start(bf16[16,33,2,128]{3,2,1,0:T(2,128)(2,1)S(1)} %all_to_all.14), channel_id=1, source_target_pairs={{0,8},{8,0},{1,9},{9,1},{2,10},{10,2},{3,11},{11,3},{4,12},{12,4},... | collective-permute-start | bytes 811016 | tf_op jit(solution)/shard_map/ppermute | solution.py:241
  26.4 20.7 %collective-permute-start.1 = (bf16[16,33,2,128]{3,2,1,0:T(2,128)(2,1)S(1)}, bf16[16,33,2,128]{3,2,1,0:T(2,128)(2,1)S(1)}, u32[]{:S(2)}, u32[]{:S(2)}) collective-permute-start(bf16[16,33,2,128]{3,2,1,0:T(2,128)(2,1)S(1)} %all_to_all.14), channel_id=1, source_target_pairs={{0,1},{1,0},{2,3},{3,2},{4,5},{5,4},{6,7},{7,6},{8,9},{9,8},{10,11... | collective-permute-start | bytes 811016 | tf_op jit(solution)/shard_map/ppermute | solution.py:242
  32.4 14.7 %collective-permute-start.2 = (bf16[16,33,2,128]{3,2,1,0:T(2,128)(2,1)S(1)}, bf16[16,33,2,128]{3,2,1,0:T(2,128)(2,1)S(1)}, u32[]{:S(2)}, u32[]{:S(2)}) collective-permute-start(bf16[16,33,2,128]{3,2,1,0:T(2,128)(2,1)S(1)} %collective-permute-done), channel_id=1, source_target_pairs={{0,1},{1,0},{2,3},{3,2},{4,5},{5,4},{6,7},{7,6},{8,9},{9,8},{10,11... | collective-permute-start | bytes 811016 | tf_op jit(solution)/shard_map/ppermute | solution.py:243
  32.4 4.9 %collective-permute-start.3 = (f32[2,512]{1,0:T(2,128)S(1)}, f32[2,512]{1,0:T(2,128)S(1)}, u32[]{:S(2)}, u32[]{:S(2)}) collective-permute-start(f32[2,512]{1,0:T(2,128)S(1)} %get-tuple-element.8.refs_0_), channel_id=1, source_target_pairs={{0,2},{2,4},{4,6},{6,0},{1,3},{3,5},{5,7},{7,1},{8,10},{10,12},{12... | collective-permute-start | bytes 12296 | tf_op jit(solution)/shard_map/ppermute | solution.py:239
  34.0 5.1 %collective-permute-start.4 = (f32[2,512]{1,0:T(2,128)S(1)}, f32[2,512]{1,0:T(2,128)S(1)}, u32[]{:S(2)}, u32[]{:S(2)}) collective-permute-start(f32[2,512]{1,0:T(2,128)S(1)} %get-tuple-element.8.refs_0_), channel_id=1, source_target_pairs={{0,4},{2,6},{4,0},{6,2},{1,5},{3,7},{5,1},{7,3},{8,12},{10,14},{12... | collective-permute-start | bytes 12296 | tf_op jit(solution)/shard_map/ppermute | solution.py:239
  34.9 4.2 %collective-permute-start.5 = (f32[2,512]{1,0:T(2,128)S(1)}, f32[2,512]{1,0:T(2,128)S(1)}, u32[]{:S(2)}, u32[]{:S(2)}) collective-permute-start(f32[2,512]{1,0:T(2,128)S(1)} %get-tuple-element.8.refs_0_), channel_id=1, source_target_pairs={{0,6},{2,0},{4,2},{6,4},{1,7},{3,1},{5,3},{7,5},{8,14},{10,8},{12,... | collective-permute-start | bytes 12296 | tf_op jit(solution)/shard_map/ppermute | solution.py:239
where the time goes:
time: 65 us; the launch traced here: 64.5 us
  blocking collectives  36.3 us (56%)
  Pallas kernels  13.6 us (21%)
  waiting for transfers between devices  7.78 us (12%)
  starting transfers between devices  6.01 us (9%)
    all_to_all x1, blocking collectives, spectrum_of(): lax.all_to_all(pieces.reshape(rows * far, *pieces.shape[2:]), (ROWS, FAR)...  24.3 us
    all_to_all x1, blocking collectives, spectrum_of(): lax.all_to_all(sums.reshape(rows * side, -1), (ROWS, SIDE), 0, 0, tiled=T...  12 us
    pallas_call x1, Pallas kernels, steering_of(): pl.pallas_call(steering_kernel, out_shape=pltpu.VMEM((2, blocks, elements...  6.66 us
    ppermute x1, waiting for transfers between devices, spectrum_of(): along = lax.ppermute(own, NEAR, [(0, 1), (1, 0)])  6.01 us
    ppermute x3, starting transfers between devices, spectrum_of(): turned.append(lax.ppermute(turns, SIDE, moves))  4.93 us
    pallas_call x1, Pallas kernels, sums_of(): pl.pallas_call(sums_kernel, out_shape=jax.ShapeDtypeStruct((blocks, LANES...  4.67 us
    ppermute x3, waiting for transfers between devices, spectrum_of(): turned.append(lax.ppermute(turns, SIDE, moves))  1.76 us
  transfers between devices with their start and end apart: 6, of which 2 were waited for; matrix products, arithmetic and copies ran while one was open for 0% of the time, Pallas kernels for 12%

commit v1 on v0

--- a/solution.py
+++ b/solution.py
@@ -11,7 +11,7 @@
 PHASES = 4096
 LATTICE = 64
 LANES = 128
-BATCH = 32
+BATCH = 128
 PITCH = BATCH + 4
 ROWS, FAR, NEAR, SIDE, CORE = "rows", "far", "near", "side", "core"
 GRID = (FAR, NEAR, SIDE, CORE)
@@ -91,11 +91,10 @@
 
 def tables_kernel(*refs):
     *parts, table_ref, turns = refs
-    side, share = len(parts), parts[0].shape[1]
-    blocks = turns.shape[1]
+    share, blocks = parts[0].shape[1], turns.shape[1]
     each = share // LANES
     for s, ref in enumerate(parts):
-        first = lax.rem(lax.axis_index(SIDE) + side - s, side) * each
+        first = (lax.axis_index(SIDE) ^ s) * each
         part = ref[...]
         for j in range(each):
             for k in range(2):
@@ -235,7 +234,7 @@
     )
     turned = [turns]
     for step in range(1, side):
-        moves = [(s, (s + step) % side) for s in range(side)]
+        moves = [(s, s ^ step) for s in range(side)]
         turned.append(lax.ppermute(turns, SIDE, moves))
     cores = [(0, 1), (1, 0)]
     along = lax.ppermute(own, NEAR, [(0, 1), (1, 0)])

time: 65 us -> 64 us (0.985)
  starting transfers between devices: 6.01 us -> 4.57 us
  waiting for transfers between devices: 7.78 us -> 9.17 us
    ppermute x3, starting transfers between devices: 4.93 us -> 3.49 us  [spectrum_of(): turned.append(lax.ppermute(turns, SIDE, moves))]
    ppermute x3, waiting for transfers between devices: 1.76 us -> 3.16 us  [spectrum_of(): turned.append(lax.ppermute(turns, SIDE, moves))]
  transfers between devices with their start and end apart: 6 -> 6, of which waited for: 2 -> 4; matrix products, arithmetic and copies ran while one was open for 0% -> 0% of each run, Pallas kernels for 12% -> 12%
where the time goes in v1:
time: 64 us; the launch traced here: 63.7 us
  blocking collectives  36.1 us (56%)
  Pallas kernels  13.1 us (20%)
  waiting for transfers between devices  9.17 us (14%)
  starting transfers between devices  4.57 us (7%)
    all_to_all x1, blocking collectives, spectrum_of(): lax.all_to_all(pieces.reshape(rows * far, *pieces.shape[2:]), (ROWS, FAR)...  24.3 us
    all_to_all x1, blocking collectives, spectrum_of(): lax.all_to_all(sums.reshape(rows * side, -1), (ROWS, SIDE), 0, 0, tiled=T...  11.8 us
    pallas_call x1, Pallas kernels, steering_of(): pl.pallas_call(steering_kernel, out_shape=pltpu.VMEM((2, blocks, elements...  6.12 us
    ppermute x1, waiting for transfers between devices, spectrum_of(): along = lax.ppermute(own, NEAR, [(0, 1), (1, 0)])  6.01 us
    pallas_call x1, Pallas kernels, sums_of(): pl.pallas_call(sums_kernel, out_shape=jax.ShapeDtypeStruct((blocks, LANES...  4.67 us
    ppermute x3, starting transfers between devices, spectrum_of(): turned.append(lax.ppermute(turns, SIDE, moves))  3.49 us
    ppermute x3, waiting for transfers between devices, spectrum_of(): turned.append(lax.ppermute(turns, SIDE, moves))  3.16 us
    pallas_call x1, Pallas kernels, tables_of(): pl.pallas_call(tables_kernel, out_shape=jax.ShapeDtypeStruct((2, LATTICE...  1.29 us
  transfers between devices with their start and end apart: 6, of which 4 were waited for; matrix products, arithmetic and copies ran while one was open for 0% of the time, Pallas kernels for 12%

profile of v1, /device:TPU:8, one launch (start us, length us, event | category | flops | bytes accessed | tf_op | source)
XLA Modules:
  0.0 63.7 jit_solution(8637031901009259309)
XLA Ops:
  0.0 1.0 %pack.1 = (bf16[4,4,33,2,128]{4,3,2,1,0:T(2,128)(2,1)S(1)}, f32[2,512]{1,0:T(2,128)S(1)}) custom-call(s32[4,2,128]{2,1,0:T(2,128)} %bitcast.16, s32[2,512]{1,0:T(2,128)} %angles_hbm.1, bf16[30,2,512]{2,1,0:T(2,128)(2,1)} %bitcast.15), custom_call_target="tpu_custom_call" | custom-call | flops 65536 | tf_op jit(solution)/shard_map/pack/pallas_call | solution.py:72
  1.0 24.3 %all_to_all.14 = bf16[16,33,2,128]{3,2,1,0:T(2,128)(2,1)S(1)} all-to-all(bf16[16,33,2,128]{3,2,1,0:T(2,128)(2,1)S(1)} %bitcast.11), channel_id=1, replica_groups=mesh['rows'=4,'far'=4,'near'=2,'side'=4,'core'=2] {'rows','far'}, dimensions={0} | all-to-all | bytes 540672 | tf_op jit(solution)/shard_map/all_to_all | solution.py:232
  25.3 1.1 %collective-permute-start = (bf16[16,33,2,128]{3,2,1,0:T(2,128)(2,1)S(1)}, bf16[16,33,2,128]{3,2,1,0:T(2,128)(2,1)S(1)}, u32[]{:S(2)}, u32[]{:S(2)}) collective-permute-start(bf16[16,33,2,128]{3,2,1,0:T(2,128)(2,1)S(1)} %all_to_all.14), channel_id=1, source_target_pairs={{0,8},{8,0},{1,9},{9,1},{2,10},{10,2},{3,11},{11,3},{4,12},{12,4},... | collective-permute-start | bytes 811016 | tf_op jit(solution)/shard_map/ppermute | solution.py:240
  26.4 0.0 collective-permute-start.1
  26.4 6.0 %collective-permute-done = bf16[16,33,2,128]{3,2,1,0:T(2,128)(2,1)S(1)} collective-permute-done((bf16[16,33,2,128]{3,2,1,0:T(2,128)(2,1)S(1)}, bf16[16,33,2,128]{3,2,1,0:T(2,128)(2,1)S(1)}, u32[]{:S(2)}, u32[]{:S(2)}) %collective-permute-start) | collective-permute-done | bytes 270368 | tf_op jit(solution)/shard_map/ppermute | solution.py:240
  32.4 0.0 collective-permute-start.2
  32.4 0.5 collective-permute-start.3
  32.9 2.6 %collective-permute-start.4 = (f32[2,512]{1,0:T(2,128)S(1)}, f32[2,512]{1,0:T(2,128)S(1)}, u32[]{:S(2)}, u32[]{:S(2)}) collective-permute-start(f32[2,512]{1,0:T(2,128)S(1)} %get-tuple-element.8.refs_0_), channel_id=1, source_target_pairs={{0,4},{2,6},{4,0},{6,2},{1,5},{3,7},{5,1},{7,3},{8,12},{10,14},{12... | collective-permute-start | bytes 12296 | tf_op jit(solution)/shard_map/ppermute | solution.py:238
  35.4 0.5 collective-permute-start.5
  35.9 0.1 collective-permute-done.3.refs_1_
  36.0 2.0 %collective-permute-done.4.refs_2_ = f32[2,512]{1,0:T(2,128)S(1)} collective-permute-done((f32[2,512]{1,0:T(2,128)S(1)}, f32[2,512]{1,0:T(2,128)S(1)}, u32[]{:S(2)}, u32[]{:S(2)}) %collective-permute-start.4) | collective-permute-done | bytes 4128 | tf_op jit(solution)/shard_map/ppermute | solution.py:238
  38.0 1.1 %collective-permute-done.5.refs_3_ = f32[2,512]{1,0:T(2,128)S(1)} collective-permute-done((f32[2,512]{1,0:T(2,128)S(1)}, f32[2,512]{1,0:T(2,128)S(1)}, u32[]{:S(2)}, u32[]{:S(2)}) %collective-permute-start.5) | collective-permute-done | bytes 4128 | tf_op jit(solution)/shard_map/ppermute | solution.py:238
  39.1 1.3 %tables.1.table_ref = f32[2,2048,128]{2,1,0:T(8,128)S(1)} custom-call(f32[2,512]{1,0:T(2,128)S(1)} %get-tuple-element.8.refs_0_, f32[2,512]{1,0:T(2,128)S(1)} %collective-permute-done.3.refs_1_, f32[2,512]{1,0:T(2,128)S(1)} %collective-permute-done.4.refs_2_, f32[2,512]{1,0:T(2,128)S(1)} %collective-permute-done.5.refs_3_), custom_call_target="tpu_custom_call" | custom-call | flops 4194304 | tf_op jit(solution)/shard_map/tables/pallas_call | solution.py:116
  40.3 6.1 %steering.1.refs_4_ = bf16[2,16,2048,128]{3,2,1,0:T(8,128)(2,1)S(1)} custom-call(bf16[4,4,33,2,128]{4,3,2,1,0:T(2,128)(2,1)S(1)} %bitcast.9, f32[2,2048,128]{2,1,0:T(8,128)S(1)} %tables.1.table_ref), custom_call_target="tpu_custom_call" | custom-call | flops 268435456 | tf_op jit(solution)/shard_map/steering/pallas_call | solution.py:163
  46.5 0.0 collective-permute-done.1
  46.5 0.0 collective-permute-done.2
  46.5 4.7 %sums.1 = f32[16,128]{1,0:T(8,128)S(1)} custom-call(bf16[4,4,33,2,128]{4,3,2,1,0:T(2,128)(2,1)S(1)} %bitcast.10, bf16[4,4,33,2,128]{4,3,2,1,0:T(2,128)(2,1)S(1)} %bitcast.12, bf16[4,4,33,2,128]{4,3,2,1,0:T(2,128)(2,1)S(1)} %bitcast.13, bf16[4,4,33,2,128]{4,3,2,1,0:T(2,128)(2,1)S(1)} %bitcast.14, bf16[2,16,2048,128]{3,2,1,0:T(8,128)(2,1)S(1)} %steering.1.refs_4_), custom_call_target="tpu_custom_call" | custom-call | flops 8858370048 | tf_op jit(solution)/shard_map/sums/pallas_call | solution.py:212
  51.2 0.1 all_to_all.10
  51.3 11.8 %all_to_all.15 = f32[16,1,512]{2,1,0:T(1,128)S(1)} all-to-all(f32[16,1,512]{2,1,0:T(1,128)S(1)} %all_to_all.10), channel_id=1, replica_groups=mesh['rows'=4,'far'=4,'near'=2,'side'=4,'core'=2] {'rows','side'}, dimensions={0} | all-to-all | bytes 65536 | tf_op jit(solution)/shard_map/all_to_all | solution.py:248
  63.1 0.6 add_divide_fusion
  (3 shorter events, 0.1 us)
Async XLA Ops:
  25.3 7.1 %collective-permute-start = (bf16[16,33,2,128]{3,2,1,0:T(2,128)(2,1)S(1)}, bf16[16,33,2,128]{3,2,1,0:T(2,128)(2,1)S(1)}, u32[]{:S(2)}, u32[]{:S(2)}) collective-permute-start(bf16[16,33,2,128]{3,2,1,0:T(2,128)(2,1)S(1)} %all_to_all.14), channel_id=1, source_target_pairs={{0,8},{8,0},{1,9},{9,1},{2,10},{10,2},{3,11},{11,3},{4,12},{12,4},... | collective-permute-start | bytes 811016 | tf_op jit(solution)/shard_map/ppermute | solution.py:240
  26.4 20.1 %collective-permute-start.1 = (bf16[16,33,2,128]{3,2,1,0:T(2,128)(2,1)S(1)}, bf16[16,33,2,128]{3,2,1,0:T(2,128)(2,1)S(1)}, u32[]{:S(2)}, u32[]{:S(2)}) collective-permute-start(bf16[16,33,2,128]{3,2,1,0:T(2,128)(2,1)S(1)} %all_to_all.14), channel_id=1, source_target_pairs={{0,1},{1,0},{2,3},{3,2},{4,5},{5,4},{6,7},{7,6},{8,9},{9,8},{10,11... | collective-permute-start | bytes 811016 | tf_op jit(solution)/shard_map/ppermute | solution.py:241
  32.4 14.1 %collective-permute-start.2 = (bf16[16,33,2,128]{3,2,1,0:T(2,128)(2,1)S(1)}, bf16[16,33,2,128]{3,2,1,0:T(2,128)(2,1)S(1)}, u32[]{:S(2)}, u32[]{:S(2)}) collective-permute-start(bf16[16,33,2,128]{3,2,1,0:T(2,128)(2,1)S(1)} %collective-permute-done), channel_id=1, source_target_pairs={{0,1},{1,0},{2,3},{3,2},{4,5},{5,4},{6,7},{7,6},{8,9},{9,8},{10,11... | collective-permute-start | bytes 811016 | tf_op jit(solution)/shard_map/ppermute | solution.py:242
  32.4 3.6 %collective-permute-start.3 = (f32[2,512]{1,0:T(2,128)S(1)}, f32[2,512]{1,0:T(2,128)S(1)}, u32[]{:S(2)}, u32[]{:S(2)}) collective-permute-start(f32[2,512]{1,0:T(2,128)S(1)} %get-tuple-element.8.refs_0_), channel_id=1, source_target_pairs={{0,2},{2,0},{4,6},{6,4},{1,3},{3,1},{5,7},{7,5},{8,10},{10,8},{12,... | collective-permute-start | bytes 12296 | tf_op jit(solution)/shard_map/ppermute | solution.py:238
  32.9 5.1 %collective-permute-start.4 = (f32[2,512]{1,0:T(2,128)S(1)}, f32[2,512]{1,0:T(2,128)S(1)}, u32[]{:S(2)}, u32[]{:S(2)}) collective-permute-start(f32[2,512]{1,0:T(2,128)S(1)} %get-tuple-element.8.refs_0_), channel_id=1, source_target_pairs={{0,4},{2,6},{4,0},{6,2},{1,5},{3,7},{5,1},{7,3},{8,12},{10,14},{12... | collective-permute-start | bytes 12296 | tf_op jit(solution)/shard_map/ppermute | solution.py:238
  35.4 3.6 %collective-permute-start.5 = (f32[2,512]{1,0:T(2,128)S(1)}, f32[2,512]{1,0:T(2,128)S(1)}, u32[]{:S(2)}, u32[]{:S(2)}) collective-permute-start(f32[2,512]{1,0:T(2,128)S(1)} %get-tuple-element.8.refs_0_), channel_id=1, source_target_pairs={{0,6},{2,4},{4,2},{6,0},{1,7},{3,5},{5,3},{7,1},{8,14},{10,12},{12... | collective-permute-start | bytes 12296 | tf_op jit(solution)/shard_map/ppermute | solution.py:238

commit v2 on v1

--- a/solution.py
+++ b/solution.py
@@ -11,7 +11,7 @@
 PHASES = 4096
 LATTICE = 64
 LANES = 128
-BATCH = 128
+BATCH = 256
 PITCH = BATCH + 4
 ROWS, FAR, NEAR, SIDE, CORE = "rows", "far", "near", "side", "core"
 GRID = (FAR, NEAR, SIDE, CORE)
@@ -134,9 +134,16 @@
             for k in range(2):
                 here = k * elements + (r * tiles + t) * LANES
                 listed[here : here + LANES] = part[k]
-    copy = pltpu.make_async_copy(listed, rows, arrived)
-    copy.start()
-    copy.wait()
+    early = BATCH * 2
+    spans = [(0, early), (elements, early), (early, elements - early), (elements + early, elements - early)]
+    copies = [
+        pltpu.make_async_copy(listed.at[pl.ds(*span)], rows.at[pl.ds(*span)], arrived.at[k])
+        for k, span in enumerate(spans)
+    ]
+    for copy in copies:
+        copy.start()
+    for copy in copies[:2]:
+        copy.wait()
 
     def batch(step, carry):
         first = pl.multiple_of(step * BATCH, BATCH)
@@ -154,7 +161,10 @@
                 out_ref[k, b, pl.ds(first, BATCH), :] = part.astype(out_ref.dtype)
         return carry
 
-    lax.fori_loop(0, elements // BATCH, batch, 0)
+    lax.fori_loop(0, early // BATCH, batch, 0)
+    for copy in copies[2:]:
+        copy.wait()
+    lax.fori_loop(early // BATCH, elements // BATCH, batch, 0)
 
 
 def steering_of(own, table):
@@ -169,7 +179,7 @@
             pltpu.VMEM((2, blocks * PITCH, LANES), jnp.float32),
             pltpu.VMEM((2 * elements,), jnp.int32),
             pltpu.SMEM((2 * elements,), jnp.int32),
-            pltpu.SemaphoreType.DMA,
+            pltpu.SemaphoreType.DMA((4,)),
         ],
         cost_estimate=pl.CostEstimate(
             flops=64 * blocks * elements * LANES, bytes_accessed=0, transcendentals=0

time: 64 us -> 63.8 us (level)
  transfers between devices with their start and end apart: 6 -> 6, of which waited for: 4 -> 4; matrix products, arithmetic and copies ran while one was open for 0% -> 0% of each run, Pallas kernels for 12% -> 11%
where the time goes in v2:
time: 63.8 us; the launch traced here: 63.5 us
  blocking collectives  36.1 us (57%)
  Pallas kernels  12.9 us (20%)
  waiting for transfers between devices  9.17 us (14%)
  starting transfers between devices  4.57 us (7%)
    all_to_all x1, blocking collectives, spectrum_of(): lax.all_to_all(pieces.reshape(rows * far, *pieces.shape[2:]), (ROWS, FAR)...  24.3 us
    all_to_all x1, blocking collectives, spectrum_of(): lax.all_to_all(sums.reshape(rows * side, -1), (ROWS, SIDE), 0, 0, tiled=T...  11.8 us
    ppermute x1, waiting for transfers between devices, spectrum_of(): along = lax.ppermute(own, NEAR, [(0, 1), (1, 0)])  6.01 us
    pallas_call x1, Pallas kernels, steering_of(): pl.pallas_call(steering_kernel, out_shape=pltpu.VMEM((2, blocks, elements...  5.92 us
    pallas_call x1, Pallas kernels, sums_of(): pl.pallas_call(sums_kernel, out_shape=jax.ShapeDtypeStruct((blocks, LANES...  4.67 us
    ppermute x3, starting transfers between devices, spectrum_of(): turned.append(lax.ppermute(turns, SIDE, moves))  3.49 us
    ppermute x3, waiting for transfers between devices, spectrum_of(): turned.append(lax.ppermute(turns, SIDE, moves))  3.16 us
    pallas_call x1, Pallas kernels, tables_of(): pl.pallas_call(tables_kernel, out_shape=jax.ShapeDtypeStruct((2, LATTICE...  1.29 us
  transfers between devices with their start and end apart: 6, of which 4 were waited for; matrix products, arithmetic and copies ran while one was open for 0% of the time, Pallas kernels for 11%

profile of v2, /device:TPU:8, one launch (start us, length us, event | category | flops | bytes accessed | tf_op | source)
XLA Modules:
  0.0 63.5 jit_solution(9384480196019761736)
XLA Ops:
  0.0 1.0 %pack.1 = (bf16[4,4,33,2,128]{4,3,2,1,0:T(2,128)(2,1)S(1)}, f32[2,512]{1,0:T(2,128)S(1)}) custom-call(s32[4,2,128]{2,1,0:T(2,128)} %bitcast.16, s32[2,512]{1,0:T(2,128)} %angles_hbm.1, bf16[30,2,512]{2,1,0:T(2,128)(2,1)} %bitcast.15), custom_call_target="tpu_custom_call" | custom-call | flops 65536 | tf_op jit(solution)/shard_map/pack/pallas_call | solution.py:72
  1.0 24.3 %all_to_all.14 = bf16[16,33,2,128]{3,2,1,0:T(2,128)(2,1)S(1)} all-to-all(bf16[16,33,2,128]{3,2,1,0:T(2,128)(2,1)S(1)} %bitcast.11), channel_id=1, replica_groups=mesh['rows'=4,'far'=4,'near'=2,'side'=4,'core'=2] {'rows','far'}, dimensions={0} | all-to-all | bytes 540672 | tf_op jit(solution)/shard_map/all_to_all | solution.py:242
  25.3 1.1 %collective-permute-start = (bf16[16,33,2,128]{3,2,1,0:T(2,128)(2,1)S(1)}, bf16[16,33,2,128]{3,2,1,0:T(2,128)(2,1)S(1)}, u32[]{:S(2)}, u32[]{:S(2)}) collective-permute-start(bf16[16,33,2,128]{3,2,1,0:T(2,128)(2,1)S(1)} %all_to_all.14), channel_id=1, source_target_pairs={{0,8},{8,0},{1,9},{9,1},{2,10},{10,2},{3,11},{11,3},{4,12},{12,4},... | collective-permute-start | bytes 811016 | tf_op jit(solution)/shard_map/ppermute | solution.py:250
  26.4 0.0 collective-permute-start.1
  26.4 6.0 %collective-permute-done = bf16[16,33,2,128]{3,2,1,0:T(2,128)(2,1)S(1)} collective-permute-done((bf16[16,33,2,128]{3,2,1,0:T(2,128)(2,1)S(1)}, bf16[16,33,2,128]{3,2,1,0:T(2,128)(2,1)S(1)}, u32[]{:S(2)}, u32[]{:S(2)}) %collective-permute-start) | collective-permute-done | bytes 270368 | tf_op jit(solution)/shard_map/ppermute | solution.py:250
  32.4 0.0 collective-permute-start.2
  32.4 0.5 collective-permute-start.3
  32.9 2.6 %collective-permute-start.4 = (f32[2,512]{1,0:T(2,128)S(1)}, f32[2,512]{1,0:T(2,128)S(1)}, u32[]{:S(2)}, u32[]{:S(2)}) collective-permute-start(f32[2,512]{1,0:T(2,128)S(1)} %get-tuple-element.8.refs_0_), channel_id=1, source_target_pairs={{0,4},{2,6},{4,0},{6,2},{1,5},{3,7},{5,1},{7,3},{8,12},{10,14},{12... | collective-permute-start | bytes 12296 | tf_op jit(solution)/shard_map/ppermute | solution.py:248
  35.4 0.5 collective-permute-start.5
  35.9 0.1 collective-permute-done.3.refs_1_
  36.0 2.0 %collective-permute-done.4.refs_2_ = f32[2,512]{1,0:T(2,128)S(1)} collective-permute-done((f32[2,512]{1,0:T(2,128)S(1)}, f32[2,512]{1,0:T(2,128)S(1)}, u32[]{:S(2)}, u32[]{:S(2)}) %collective-permute-start.4) | collective-permute-done | bytes 4128 | tf_op jit(solution)/shard_map/ppermute | solution.py:248
  38.0 1.1 %collective-permute-done.5.refs_3_ = f32[2,512]{1,0:T(2,128)S(1)} collective-permute-done((f32[2,512]{1,0:T(2,128)S(1)}, f32[2,512]{1,0:T(2,128)S(1)}, u32[]{:S(2)}, u32[]{:S(2)}) %collective-permute-start.5) | collective-permute-done | bytes 4128 | tf_op jit(solution)/shard_map/ppermute | solution.py:248
  39.1 1.3 %tables.1.table_ref = f32[2,2048,128]{2,1,0:T(8,128)S(1)} custom-call(f32[2,512]{1,0:T(2,128)S(1)} %get-tuple-element.8.refs_0_, f32[2,512]{1,0:T(2,128)S(1)} %collective-permute-done.3.refs_1_, f32[2,512]{1,0:T(2,128)S(1)} %collective-permute-done.4.refs_2_, f32[2,512]{1,0:T(2,128)S(1)} %collective-permute-done.5.refs_3_), custom_call_target="tpu_custom_call" | custom-call | flops 4194304 | tf_op jit(solution)/shard_map/tables/pallas_call | solution.py:116
  40.3 5.9 %steering.1.refs_4_ = bf16[2,16,2048,128]{3,2,1,0:T(8,128)(2,1)S(1)} custom-call(bf16[4,4,33,2,128]{4,3,2,1,0:T(2,128)(2,1)S(1)} %bitcast.9, f32[2,2048,128]{2,1,0:T(8,128)S(1)} %tables.1.table_ref), custom_call_target="tpu_custom_call" | custom-call | flops 268435456 | tf_op jit(solution)/shard_map/steering/pallas_call | solution.py:173
  46.3 0.0 collective-permute-done.1
  46.3 0.0 collective-permute-done.2
  46.3 4.7 %sums.1 = f32[16,128]{1,0:T(8,128)S(1)} custom-call(bf16[4,4,33,2,128]{4,3,2,1,0:T(2,128)(2,1)S(1)} %bitcast.10, bf16[4,4,33,2,128]{4,3,2,1,0:T(2,128)(2,1)S(1)} %bitcast.12, bf16[4,4,33,2,128]{4,3,2,1,0:T(2,128)(2,1)S(1)} %bitcast.13, bf16[4,4,33,2,128]{4,3,2,1,0:T(2,128)(2,1)S(1)} %bitcast.14, bf16[2,16,2048,128]{3,2,1,0:T(8,128)(2,1)S(1)} %steering.1.refs_4_), custom_call_target="tpu_custom_call" | custom-call | flops 8858370048 | tf_op jit(solution)/shard_map/sums/pallas_call | solution.py:222
  51.0 0.1 all_to_all.10
  51.0 11.8 %all_to_all.15 = f32[16,1,512]{2,1,0:T(1,128)S(1)} all-to-all(f32[16,1,512]{2,1,0:T(1,128)S(1)} %all_to_all.10), channel_id=1, replica_groups=mesh['rows'=4,'far'=4,'near'=2,'side'=4,'core'=2] {'rows','side'}, dimensions={0} | all-to-all | bytes 65536 | tf_op jit(solution)/shard_map/all_to_all | solution.py:258
  62.9 0.6 add_divide_fusion
  (3 shorter events, 0.1 us)
Async XLA Ops:
  25.3 7.1 %collective-permute-start = (bf16[16,33,2,128]{3,2,1,0:T(2,128)(2,1)S(1)}, bf16[16,33,2,128]{3,2,1,0:T(2,128)(2,1)S(1)}, u32[]{:S(2)}, u32[]{:S(2)}) collective-permute-start(bf16[16,33,2,128]{3,2,1,0:T(2,128)(2,1)S(1)} %all_to_all.14), channel_id=1, source_target_pairs={{0,8},{8,0},{1,9},{9,1},{2,10},{10,2},{3,11},{11,3},{4,12},{12,4},... | collective-permute-start | bytes 811016 | tf_op jit(solution)/shard_map/ppermute | solution.py:250
  26.4 19.9 %collective-permute-start.1 = (bf16[16,33,2,128]{3,2,1,0:T(2,128)(2,1)S(1)}, bf16[16,33,2,128]{3,2,1,0:T(2,128)(2,1)S(1)}, u32[]{:S(2)}, u32[]{:S(2)}) collective-permute-start(bf16[16,33,2,128]{3,2,1,0:T(2,128)(2,1)S(1)} %all_to_all.14), channel_id=1, source_target_pairs={{0,1},{1,0},{2,3},{3,2},{4,5},{5,4},{6,7},{7,6},{8,9},{9,8},{10,11... | collective-permute-start | bytes 811016 | tf_op jit(solution)/shard_map/ppermute | solution.py:251
  32.4 13.9 %collective-permute-start.2 = (bf16[16,33,2,128]{3,2,1,0:T(2,128)(2,1)S(1)}, bf16[16,33,2,128]{3,2,1,0:T(2,128)(2,1)S(1)}, u32[]{:S(2)}, u32[]{:S(2)}) collective-permute-start(bf16[16,33,2,128]{3,2,1,0:T(2,128)(2,1)S(1)} %collective-permute-done), channel_id=1, source_target_pairs={{0,1},{1,0},{2,3},{3,2},{4,5},{5,4},{6,7},{7,6},{8,9},{9,8},{10,11... | collective-permute-start | bytes 811016 | tf_op jit(solution)/shard_map/ppermute | solution.py:252
  32.4 3.6 %collective-permute-start.3 = (f32[2,512]{1,0:T(2,128)S(1)}, f32[2,512]{1,0:T(2,128)S(1)}, u32[]{:S(2)}, u32[]{:S(2)}) collective-permute-start(f32[2,512]{1,0:T(2,128)S(1)} %get-tuple-element.8.refs_0_), channel_id=1, source_target_pairs={{0,2},{2,0},{4,6},{6,4},{1,3},{3,1},{5,7},{7,5},{8,10},{10,8},{12,... | collective-permute-start | bytes 12296 | tf_op jit(solution)/shard_map/ppermute | solution.py:248
  32.9 5.1 %collective-permute-start.4 = (f32[2,512]{1,0:T(2,128)S(1)}, f32[2,512]{1,0:T(2,128)S(1)}, u32[]{:S(2)}, u32[]{:S(2)}) collective-permute-start(f32[2,512]{1,0:T(2,128)S(1)} %get-tuple-element.8.refs_0_), channel_id=1, source_target_pairs={{0,4},{2,6},{4,0},{6,2},{1,5},{3,7},{5,1},{7,3},{8,12},{10,14},{12... | collective-permute-start | bytes 12296 | tf_op jit(solution)/shard_map/ppermute | solution.py:248
  35.4 3.6 %collective-permute-start.5 = (f32[2,512]{1,0:T(2,128)S(1)}, f32[2,512]{1,0:T(2,128)S(1)}, u32[]{:S(2)}, u32[]{:S(2)}) collective-permute-start(f32[2,512]{1,0:T(2,128)S(1)} %get-tuple-element.8.refs_0_), channel_id=1, source_target_pairs={{0,6},{2,4},{4,2},{6,0},{1,7},{3,5},{5,3},{7,1},{8,14},{10,12},{12... | collective-permute-start | bytes 12296 | tf_op jit(solution)/shard_map/ppermute | solution.py:248
